TPU v7x, 8 devices: a whole 2x2x1 slice. The times are simulated.
8 devices in a mesh: dp: 1 (over z), ep2: 2 (over y), ep: 4 (over x, core).
Axes of the slice: x: 2, y: 2, z: 1, core: 2. Of those that a mesh axis runs over, the one named last changes fastest.
Arguments:
- x_tok: bfloat16 [16384, 768], P(('dp', 'ep2', 'ep'))
- expert_ids: int32 [16384, 1], P(('dp', 'ep2', 'ep'))
- gate_w: float32 [16384, 1], P(('dp', 'ep2', 'ep'))
- w_in: bfloat16 [128, 768, 3072], P(('ep2', 'ep'))
- w_out: bfloat16 [128, 3072, 768], P(('ep2', 'ep'))
Outputs:
- output: bfloat16 [16384, 768], P(('dp', 'ep2', 'ep'))
All inputs are finite; a program needn't handle non-finite values.
Results may differ from a plain program's by a relative error of at most 0.001.
Values are sent between devices in bfloat16 or wider.
A program may use at most 1 GiB of HBM per device.

v0:
```python
import jax
import jax.numpy as jnp
from jax import lax
from jax.sharding import PartitionSpec as P


def slot_sizes(group_size, n_tok, n_top, experts):
    capacity = 8 * ((5 * group_size * n_tok * n_top) // (32 * experts))
    lane_max = 2 * ((n_tok * n_top) // experts) - 1
    return capacity, lane_max


def pack_rows(x_loc, flat_e, counts, offsets, capacity, lane_max):
    n_tok = x_loc.shape[0]
    n_pair = flat_e.shape[0]
    pair_order = jnp.argsort(flat_e, stable=True)
    starts = jnp.cumsum(counts) - counts
    kept_n = jnp.clip(capacity - offsets, 0, counts)
    lane_ids = jnp.arange(lane_max)
    src_pair = pair_order[jnp.minimum(starts[:, None] + lane_ids[None, :], n_pair - 1)]
    is_kept = lane_ids[None, :] < kept_n[:, None]
    send_rows = jnp.where(is_kept[:, :, None], x_loc[src_pair // (n_pair // n_tok)], jnp.zeros((), x_loc.dtype))
    sorted_rank = jnp.arange(n_pair) - starts[flat_e[pair_order]]
    pair_rank = jnp.zeros((n_pair,), jnp.int32).at[pair_order].set(sorted_rank)
    return send_rows, pair_rank, kept_n


def expert_rows(recv_rows, src_counts, src_offsets, w_a, w_b, capacity):
    group_size, e_loc, lane_max, d_model = recv_rows.shape
    range_end = src_offsets + src_counts
    totals = jnp.sum(src_counts, axis=0)
    slot_ids = jnp.arange(capacity)
    src_dev = jnp.sum((range_end[:, :, None] <= slot_ids[None, None, :]).astype(jnp.int32), axis=0)
    src_dev = jnp.minimum(src_dev, group_size - 1)
    expert_pos = jnp.arange(e_loc)[:, None]
    slot_base = jnp.take_along_axis(src_offsets.T, src_dev, axis=1)
    lane_pos = jnp.clip(slot_ids[None, :] - slot_base, 0, lane_max - 1)
    flat_pos = (src_dev * e_loc + expert_pos) * lane_max + lane_pos
    filled = slot_ids[None, :] < totals[:, None]
    gathered = recv_rows.reshape(group_size * e_loc * lane_max, d_model)[flat_pos]
    slot_rows = jnp.where(filled[:, :, None], gathered, jnp.zeros((), recv_rows.dtype))
    hidden = jax.nn.gelu(jnp.einsum('ecd,edf->ecf', slot_rows, w_a, preferred_element_type=jnp.float32), approximate=True).astype(jnp.bfloat16)
    out_rows = jnp.einsum('ecf,efd->ecd', hidden, w_b, preferred_element_type=jnp.float32).astype(jnp.bfloat16)
    back_pos = expert_pos[None] * capacity + jnp.clip(src_offsets[:, :, None] + jnp.arange(lane_max)[None, None, :], 0, capacity - 1)
    return out_rows.reshape(e_loc * capacity, d_model)[back_pos]


def combine_rows(x_loc, back_rows, flat_e, flat_gate, pair_rank, kept_n):
    n_tok, d_model = x_loc.shape
    experts, lane_max, _ = back_rows.shape
    n_top = flat_e.shape[0] // n_tok
    got_rows = back_rows.reshape(experts * lane_max, d_model)[flat_e * lane_max + pair_rank]
    weight = jnp.where(pair_rank < kept_n[flat_e], flat_gate, 0.0)
    mix_sum = jnp.sum((weight[:, None] * got_rows.astype(jnp.float32)).reshape(n_tok, n_top, d_model), axis=1)
    return (x_loc.astype(jnp.float32) + mix_sum).astype(jnp.bfloat16)


def solution(mesh):
    dev_axes = ('ep2', 'ep')
    group_size = mesh.shape['ep2'] * mesh.shape['ep']

    def local_step(x_loc, ids_loc, gate_loc, w_a, w_b):
        n_tok, d_model = x_loc.shape
        n_top = ids_loc.shape[1]
        e_loc = w_a.shape[0]
        experts = e_loc * group_size
        capacity, lane_max = slot_sizes(group_size, n_tok, n_top, experts)
        flat_e = ids_loc.reshape(-1)
        counts = jnp.bincount(flat_e, length=experts)
        src_counts = lax.all_to_all(counts.reshape(group_size, e_loc), dev_axes, 0, 0, tiled=True)
        src_offsets = jnp.cumsum(src_counts, axis=0) - src_counts
        offsets = lax.all_to_all(src_offsets, dev_axes, 0, 0, tiled=True).reshape(experts)
        send_rows, pair_rank, kept_n = pack_rows(x_loc, flat_e, counts, offsets, capacity, lane_max)
        recv_rows = lax.all_to_all(send_rows.reshape(group_size, e_loc, lane_max, d_model), dev_axes, 0, 0, tiled=True)
        out_rows = expert_rows(recv_rows, src_counts, src_offsets, w_a, w_b, capacity)
        back_rows = lax.all_to_all(out_rows, dev_axes, 0, 0, tiled=True).reshape(experts, lane_max, d_model)
        return combine_rows(x_loc, back_rows, flat_e, gate_loc.reshape(-1), pair_rank, kept_n)

    tok_spec = P(('dp', 'ep2', 'ep'), None)
    w_spec = P(dev_axes, None, None)
    return jax.shard_map(local_step, mesh=mesh, in_specs=(tok_spec, tok_spec, tok_spec, w_spec, w_spec), out_specs=tok_spec, check_vma=False)
```

profile of v0, /device:TPU:0, one launch (start us, length us, event | category | flops | bytes accessed | tf_op | source)
XLA Modules:
  0.0 386.0 jit_solution(18164076827272939062)
XLA Ops:
  1.3 14.7 %scatter_custom_fusion = s32[128]{0:T(128)S(1)} fusion(s32[2048]{0:T(1024)S(1)} %bitcast.61, s32[2048]{0:T(1024)S(1)} %broadcast.328, s32[]{:T(128)} %constant.21.clone.1), kind=kCustom, calls=%fused_computation.66 | custom fusion | flops 2048 | bytes 516 | tf_op jit(solution)/shard_map/scatter-add | solution.py:69
  16.0 8.8 %all_to_all.28 = s32[8,1,16]{2,1,0:T(1,128)S(1)} all-to-all(s32[8,1,16]{2,1,0:T(1,128)S(1)} %bitcast.60), channel_id=1, replica_groups=mesh['dp'=1,'ep2'=2,'ep'=4] {'ep2','ep'}, dimensions={0} | all-to-all | bytes 1024 | tf_op jit(solution)/shard_map/all_to_all | solution.py:70
  28.0 5.7 %sort.17 = (s32[2048]{0:T(1024)}, s32[2048]{0:T(1024)S(1)}) sort(s32[2048]{0:T(1024)} %bitcast.49, s32[2048]{0:T(1024)S(1)} %iota.45), dimensions={0}, to_apply=%region_0.1 | sort | flops 22528 | bytes 32768 | tf_op jit(solution)/shard_map/jit(argsort)/sort | solution.py:16
  34.7 20.9 %gather_fusion.3 = s32[3968]{0:T(1024)S(1)} fusion(s32[2048]{0:T(1024)S(1)} %get-tuple-element.6, s32[4096]{0:T(1024)S(1)} %pad_clamp_fusion.2), kind=kCustom, calls=%fused_computation.3 | custom fusion | bytes 47616 | tf_op jit(solution)/shard_map/gather | solution.py:20
  56.0 13.0 %gather_fusion.4 = bf16[3968,768]{1,0:T(8,128)(2,1)} fusion(bf16[2048,768]{1,0:T(8,128)(2,1)S(1)} %copy-done.3, s32[4096]{0:T(1024)S(1)} %pad_clamp_fusion.1), kind=kCustom, calls=%fused_computation.4 | custom fusion | bytes 12205568 | tf_op jit(solution)/shard_map/gather | solution.py:22
  68.9 8.5 %gather.43 = bf16[8,16,31,768]{3,2,1,0:T(8,128)(2,1)} reshape(bf16[3968,768]{1,0:T(8,128)(2,1)} %gather_fusion.4) | data formatting | bytes 12189696 | tf_op jit(solution)/shard_map/gather | solution.py:22
  81.4 6.4 %copy.20 = bf16[8,16,31,768]{3,1,2,0:T(8,128)(2,1)} copy(bf16[8,16,31,768]{3,2,1,0:T(8,128)(2,1)S(1)} %broadcast_select_fusion) | data formatting | bytes 12189696 | tf_op jit(solution)/shard_map/jit(_where)/select_n | solution.py:22
  91.7 11.1 %gather_fusion.8 = s32[2560]{0:T(1024)S(1)} fusion(s32[16,8]{0,1:T(8,128)S(1)} %bitcast.48, s32[2560]{0:T(1024)S(1)} %reshape.367), kind=kCustom, calls=%fused_computation.8 | custom fusion | bytes 40960 | tf_op jit(solution)/shard_map/jit(take_along_axis)/gather | solution.py:36
  103.4 57.4 %all-to-all-done.2 = bf16[8,16,31,768]{3,1,2,0:T(8,128)(2,1)} async-done(((bf16[8,16,31,768]{3,1,2,0:T(8,128)(2,1)}), bf16[8,16,31,768]{3,1,2,0:T(8,128)(2,1)}, u32[]{:S(2)}, u32[]{:S(2)}) %all-to-all-start.2) | async-done | bytes 6094880 | tf_op jit(solution)/shard_map/all_to_all | solution.py:74
  160.8 7.7 %copy.21 = bf16[8,16,31,768]{3,2,1,0:T(8,128)(2,1)} copy(bf16[8,16,31,768]{3,1,2,0:T(8,128)(2,1)} %all-to-all-done.2) | data formatting | bytes 12189696 | tf_op jit(solution)/shard_map/all_to_all | solution.py:74
  168.5 8.4 %reshape.301 = bf16[3968,768]{1,0:T(8,128)(2,1)} reshape(bf16[8,16,31,768]{3,2,1,0:T(8,128)(2,1)} %copy.21) | data formatting | bytes 12189696 | tf_op jit(solution)/shard_map/reshape | solution.py:40
  176.9 13.8 %gather_fusion.5 = bf16[2560,768]{1,0:T(8,128)(2,1)} fusion(bf16[3968,768]{1,0:T(8,128)(2,1)} %reshape.301, s32[3072]{0:T(1024)S(1)} %pad_clamp_fusion.3), kind=kCustom, calls=%fused_computation.5 | custom fusion | bytes 7874560 | tf_op jit(solution)/shard_map/gather | solution.py:40
  190.7 52.2 %fusion.22 = bf16[16,160,768]{2,1,0:T(8,128)(2,1)} fusion(bf16[16,3072,768]{2,1,0:T(8,128)(2,1)} %param.9, bf16[16,768,3072]{2,1,0:T(8,128)(2,1)} %param.8, bf16[16,160,768]{2,1,0:T(8,128)(2,1)} %bitcast.53, pred[16,160]{1,0:T(8,128)(4,1)S(1)} %iota_compare_fusion.2), kind=kOutput, calls=%fused_computation.30 | convolution fusion | flops 24233902080 | bytes 158861824 | tf_op jit(solution)/shard_map/ecf,efd->ecd/dot_general | solution.py:43
  242.9 18.3 %gather_fusion.6 = bf16[3968,768]{1,0:T(8,128)(2,1)} fusion(bf16[2560,768]{1,0:T(8,128)(2,1)} %bitcast.52, s32[4096]{0:T(1024)S(1)} %pad_clamp_fusion), kind=kCustom, calls=%fused_computation.6 | custom fusion | bytes 12205568 | tf_op jit(solution)/shard_map/gather | solution.py:45
  261.2 8.5 %reshape.352 = bf16[8,16,31,768]{3,2,1,0:T(8,128)(2,1)} reshape(bf16[3968,768]{1,0:T(8,128)(2,1)} %gather_fusion.6) | data formatting | bytes 12189696 | tf_op jit(solution)/shard_map/gather | solution.py:45
  269.7 9.1 %copy.22 = bf16[8,16,31,768]{3,1,2,0:T(8,128)(2,1)} copy(bf16[8,16,31,768]{3,2,1,0:T(8,128)(2,1)} %reshape.352) | data formatting | bytes 12189696 | tf_op jit(solution)/shard_map/gather | solution.py:45
  282.4 11.8 %gather_fusion = s32[2048]{0:T(1024)S(1)} fusion(s32[2048]{0:T(1024)S(1)} %bitcast.50, s32[2048]{0:T(1024)S(1)} %get-tuple-element.9), kind=kCustom, calls=%fused_computation | custom fusion | bytes 24576 | tf_op jit(solution)/shard_map/gather | solution.py:23
  294.3 12.6 %gather_fusion.1 = s32[2048]{0:T(1024)S(1)} fusion(s32[128]{0:T(128)S(1)} %copy-done.1, s32[2048]{0:T(1024)S(1)} %broadcast_clamp_fusion.1), kind=kCustom, calls=%fused_computation.1 | custom fusion | bytes 24576 | tf_op jit(solution)/shard_map/gather | solution.py:23
  306.9 12.6 %gather_fusion.2 = s32[2048]{0:T(1024)S(1)} fusion(s32[128]{0:T(128)S(1)} %get-tuple-element.11, s32[2048]{0:T(1024)S(1)} %broadcast_clamp_fusion), kind=kCustom, calls=%fused_computation.2 | custom fusion | bytes 24576 | tf_op jit(solution)/shard_map/gather | solution.py:53
  319.5 8.0 %scatter_custom_fusion.1 = s32[2048]{0:T(1024)S(1)} fusion(s32[2048]{0:T(1024)S(1)} %get-tuple-element.10, s32[2048]{0:T(1024)S(1)} %iota_subtract_fusion, s32[]{:T(128)} %constant.21.clone.1), kind=kCustom, calls=%fused_computation.63 | custom fusion | bytes 8196 | tf_op jit(solution)/shard_map/scatter | solution.py:24
  327.6 24.1 %all-to-all-done.3 = bf16[8,16,31,768]{3,1,2,0:T(8,128)(2,1)} async-done(((bf16[8,16,31,768]{3,1,2,0:T(8,128)(2,1)}), bf16[8,16,31,768]{3,1,2,0:T(8,128)(2,1)}, u32[]{:S(2)}, u32[]{:S(2)}) %all-to-all-start.3) | async-done | bytes 6094880 | tf_op jit(solution)/shard_map/all_to_all | solution.py:76
  351.7 7.7 %copy.23 = bf16[8,16,31,768]{3,2,1,0:T(8,128)(2,1)} copy(bf16[8,16,31,768]{3,1,2,0:T(8,128)(2,1)} %all-to-all-done.3) | data formatting | bytes 12189696 | tf_op jit(solution)/shard_map/all_to_all | solution.py:76
  359.5 8.4 %reshape_reshape.3 = bf16[3968,768]{1,0:T(8,128)(2,1)} reshape(bf16[8,16,31,768]{3,2,1,0:T(8,128)(2,1)} %copy.23) | data formatting | bytes 12189696 | tf_op jit(solution)/shard_map/reshape;reshape | solution.py:52
  367.9 13.6 %gather_fusion.7 = bf16[2048,768]{1,0:T(8,128)(2,1)} fusion(bf16[3968,768]{1,0:T(8,128)(2,1)} %reshape_reshape.3, s32[2048]{0:T(1024)S(1)} %fusion.32), kind=kCustom, calls=%fused_computation.7 | custom fusion | bytes 6299648 | tf_op jit(solution)/shard_map/gather | solution.py:52
  (60 shorter events, 22.4 us)
Async XLA Ops:
  25.5 8.2 %all-to-all-start.1 = ((s32[8,1,16]{2,1,0:T(1,128)}), s32[8,1,16]{2,1,0:T(1,128)S(1)}, u32[]{:S(2)}, u32[]{:S(2)}) async-start(s32[8,1,16]{2,1,0:T(1,128)} %bitcast.9), calls=%async_computation.1 | async-start | bytes 8192 | tf_op jit(solution)/shard_map/all_to_all | solution.py:72
  33.8 0.5 copy-start
  34.6 21.3 %copy-start.3 = (bf16[2048,768]{1,0:T(8,128)(2,1)S(1)}, bf16[2048,768]{1,0:T(8,128)(2,1)}, u32[]{:S(2)}) copy-start(bf16[2048,768]{1,0:T(8,128)(2,1)} %param.5) | copy-start | bytes 9437188
  87.8 72.9 %all-to-all-start.2 = ((bf16[8,16,31,768]{3,1,2,0:T(8,128)(2,1)}), bf16[8,16,31,768]{3,1,2,0:T(8,128)(2,1)}, u32[]{:S(2)}, u32[]{:S(2)}) async-start(bf16[8,16,31,768]{3,1,2,0:T(8,128)(2,1)} %copy.20), calls=%async_computation.2 | async-start | bytes 12189696 | tf_op jit(solution)/shard_map/all_to_all | solution.py:74
  278.8 3.6 copy-start.2
  278.8 73.0 %all-to-all-start.3 = ((bf16[8,16,31,768]{3,1,2,0:T(8,128)(2,1)}), bf16[8,16,31,768]{3,1,2,0:T(8,128)(2,1)}, u32[]{:S(2)}, u32[]{:S(2)}) async-start(bf16[8,16,31,768]{3,1,2,0:T(8,128)(2,1)} %copy.22), calls=%async_computation.3 | async-start | bytes 12189696 | tf_op jit(solution)/shard_map/all_to_all | solution.py:76
  282.4 11.9 %copy-start.4 = (s32[2048,1]{0,1:T(1,128)S(1)}, s32[2048,1]{0,1:T(1,128)}, u32[]{:S(2)}) copy-start(s32[2048,1]{0,1:T(1,128)} %get-tuple-element.7) | copy-start | bytes 24580
  282.4 11.9 %copy-start.1 = (s32[128]{0:T(128)S(1)}, s32[128]{0:T(128)}, u32[]{:S(2)}) copy-start(s32[128]{0:T(128)} %copy-done) | copy-start | bytes 1540
  306.9 20.7 %copy-start.5 = (f32[2048,1]{0,1:T(1,128)S(1)}, f32[2048,1]{0,1:T(1,128)}, u32[]{:S(2)}) copy-start(f32[2048,1]{0,1:T(1,128)} %param.7) | copy-start | bytes 24580
where the time goes:
time: 387 us; the launch traced here: 386 us
  local copies, waits for them, and re-layouts  202 us (52%)
  waiting for transfers between devices  81.5 us (21%)
  matrix products  52.2 us (13%)
  other arithmetic  31.6 us (8%)
  starting transfers between devices  9.29 us (2%)
  blocking collectives  8.82 us (2%)
    all_to_all x1, waiting for transfers between devices, local_step(): lax.all_to_all(send_rows.reshape(group_size, e_loc, lane_max, d_model), d...  57.4 us
    dot_general x1, matrix products, expert_rows(): jnp.einsum('ecf,efd->ecd', hidden, w_b, preferred_element_type=jnp.float32)  52.2 us
    gather x3, local copies, waits for them, and re-layouts, expert_rows(): return out_rows.reshape(e_loc * capacity, d_model)[back_pos]  35.9 us
    gather x2, local copies, waits for them, and re-layouts, pack_rows(): sorted_rank = jnp.arange(n_pair) - starts[flat_e[pair_order]]  24.4 us
    all_to_all x1, waiting for transfers between devices, local_step(): lax.all_to_all(out_rows, dev_axes, 0, 0, tiled=True)  24.1 us
    gather x2, local copies, waits for them, and re-layouts, pack_rows(): x_loc[src_pair // (n_pair // n_tok)]  21.4 us
    gather x2, local copies, waits for them, and re-layouts, pack_rows(): pair_order[jnp.minimum(starts[:, None] + lane_ids[None, :], n_pair - 1)]  21.1 us
    scatter-add x1, other arithmetic, local_step(): counts = jnp.bincount(flat_e, length=experts)  14.7 us
  transfers between devices with their start and end apart: 3, of which 2 were waited for; matrix products, arithmetic and copies ran while one was open for 16% of the time, Pallas kernels for 0%

commit v1 on v0

v1 whole, which is shorter than its diff:
```python
import functools

import jax
import jax.numpy as jnp
from jax import lax
from jax.experimental import pallas as pl
from jax.experimental.pallas import tpu as pltpu
from jax.sharding import PartitionSpec as P

MESH = pl.DeviceIdType.MESH
F32 = jnp.float32
BF16 = jnp.bfloat16
GROUP = 8
SPAN = 640
ZROWS = 48
FTILE = 1536


class Plan:
    def __init__(self, chunks, slots, need, need_lo, free, free_lo):
        self.chunks, self.slots = chunks, slots
        self.need, self.need_lo, self.free, self.free_lo = need, need_lo, free, free_lo
        for g in range(4):
            assert need_lo(g) == (need(g - 1) if g else 0)
            assert free_lo(g) == (free(g - 1) if g else 0)
            assert free(g) == chunks - (need(2 - g) if g < 3 else 0)
        assert need(3) == chunks

    def caps(self):
        return [self.need(g) * ZROWS for g in range(4)]


PLANS = (
    Plan(7, 4, lambda g: 3 + g + g // 2, lambda g: 2 * ((g + 2) // 3) + g + g // 3,
         lambda g: 1 + 2 * g - g // 2 + g // 3, lambda g: g + g // 2),
    Plan(8, 4, lambda g: 3 + 2 * g - g // 3, lambda g: 2 * g + (g + 2) // 3,
         lambda g: 1 + 2 * g + g // 3, lambda g: 2 * g - (g + 2) // 3),
    Plan(11, 3, lambda g: 3 + 3 * g - g // 2, lambda g: 3 * g - g // 3,
         lambda g: 3 + 2 * g + g // 2 + g // 3, lambda g: 3 * g - g // 2),
)


def position():
    ep = lax.axis_index('ep')
    return lax.axis_index('ep2'), ep // 2, ep % 2


def partner(where, k):
    y, x, c = where
    py = (y + k // 4) % 2
    px = (x + (k // 2) % 2) % 2
    pc = (c + k % 2) % 2
    return py * 4 + px * 2 + pc, {'ep2': py, 'ep': px * 2 + pc}


def greet(where):
    barrier = pltpu.get_barrier_semaphore()
    for k in range(1, GROUP):
        pl.semaphore_signal(barrier, inc=1, device_id=partner(where, k)[1], device_id_type=MESH)
    pl.semaphore_wait(barrier, GROUP - 1)


def route_kernel(capacity, ids_ref, gate_ref, qrow_ref, qcol_ref, dl_ref, dr_ref, sel_ref,
                 cbuf, kept_ref, off_ref, start_ref, tot_ref, mat_ref, mat_t, rank_ref, wide_ref, drow_ref,
                 send_sem, recv_sem):
    where = position()
    me = where[0] * 4 + where[1] * 2 + where[2]
    n_tok = ids_ref.shape[1]
    experts = 128
    e_loc = experts // GROUP

    hot = jnp.where(lax.broadcasted_iota(jnp.int32, (experts, n_tok), 0) == ids_ref[...], 1.0, 0.0).astype(BF16)
    cbuf[0] = lax.dot_general(jnp.ones((8, n_tok), BF16), hot, (((1,), (1,)), ((), ())), preferred_element_type=F32)

    greet(where)

    def count_copy(k):
        return pltpu.make_async_remote_copy(
            src_ref=cbuf.at[0], dst_ref=cbuf.at[k], send_sem=send_sem.at[k], recv_sem=recv_sem.at[k],
            device_id=partner(where, k)[1], device_id_type=MESH)

    for k in range(1, GROUP):
        count_copy(k).start()

    blk = 256
    upper = jnp.where(lax.broadcasted_iota(jnp.int32, (blk, blk), 0) < lax.broadcasted_iota(jnp.int32, (blk, blk), 1), 1.0, 0.0).astype(BF16)
    base = jnp.zeros((experts, 1), F32)
    for b in range(n_tok // blk):
        hot_b = hot[:, b * blk:(b + 1) * blk]
        rank_ref[:, b * blk:(b + 1) * blk] = jnp.dot(hot_b, upper, preferred_element_type=F32) + base
        base = base + jnp.sum(hot_b.astype(F32), axis=1, keepdims=True)

    for k in range(1, GROUP):
        count_copy(k).wait_recv()

    run = jnp.zeros((1, experts), F32)
    for s in range(GROUP):
        k = ((where[0] + s // 4) % 2) * 4 + ((where[1] + (s // 2) % 2) % 2) * 2 + (where[2] + s % 2) % 2
        cnt = cbuf[k, 0:1, :]
        off_ref[s:s + 1, :] = run
        kept_ref[s:s + 1, :] = jnp.minimum(jnp.maximum(capacity - run, 0.0), cnt)
        run = run + cnt
    kept = kept_ref[...]
    row_e = lax.broadcasted_iota(jnp.int32, (experts, experts), 0)
    col_e = lax.broadcasted_iota(jnp.int32, (experts, experts), 1)
    same = (row_e // e_loc) == (col_e // e_loc)
    before = jnp.where(same & (row_e < col_e), 1.0, 0.0).astype(BF16)
    block = jnp.where(same, 1.0, 0.0).astype(BF16)
    start = jnp.dot(kept.astype(BF16), before, preferred_element_type=F32)
    total = jnp.dot(kept.astype(BF16), block, preferred_element_type=F32)
    start_ref[...] = start
    tot_ref[...] = total

    last = lax.broadcasted_iota(jnp.int32, (8, experts), 1) % e_loc
    head = start + kept
    tail = total - head
    choice = jnp.zeros((8, experts), F32)
    for plan in PLANS[:-1]:
        caps = plan.caps()
        over = jnp.where(total > caps[3], 1.0, 0.0)
        for g in range(3):
            over = jnp.maximum(over, jnp.where((last == 4 * g + 3) & (head > caps[g]), 1.0, 0.0))
            over = jnp.maximum(over, jnp.where((last == 4 * g + 3) & (tail > caps[2 - g]), 1.0, 0.0))
        choice = choice + jnp.max(over, keepdims=True)
    sel_ref[...] = choice.astype(jnp.int32)

    mat_ref[...] = jnp.zeros_like(mat_ref)
    lane_k = jnp.bitwise_xor(lax.broadcasted_iota(jnp.int32, (1, experts), 1) // e_loc, me).astype(F32)
    my_start = start_ref[pl.ds(me, 1), :]
    my_code = lane_k * SPAN + my_start
    mat_ref[0:1, :] = kept_ref[pl.ds(me, 1), :]
    mat_ref[1:2, :] = my_code + 1.0
    mat_ref[2:3, :] = my_code + (SPAN + 1.0) - tot_ref[pl.ds(me, 1), :]
    for k in range(GROUP):
        s = partner(where, k)[0]
        mat_ref[8 + k:9 + k, :] = kept_ref[pl.ds(s, 1), :]
        mat_ref[16 + k:17 + k, :] = off_ref[pl.ds(s, 1), :]
        mat_ref[24 + k:25 + k, :] = start_ref[pl.ds(s, 1), :]
        mat_ref[32 + k:33 + k, :] = tot_ref[pl.ds(s, 1), :]
    mat_t[...] = jnp.transpose(mat_ref[...])

    wide_ref[...] = jnp.zeros_like(wide_ref)
    hot_f = hot.astype(F32)
    rank = rank_ref[...]
    live = jnp.where(rank < mat_t[:, 0:1], hot_f, 0.0)
    qrow_ref[...] = jnp.broadcast_to(jnp.sum(live * (rank + mat_t[:, 1:2]), axis=0, keepdims=True) - 1.0, qrow_ref.shape)
    wide_ref[0:1, :] = jnp.sum(live * (rank + mat_t[:, 2:3]), axis=0, keepdims=True) - 1.0
    wide_ref[1:2, :] = gate_ref[...]
    qcol_ref[...] = jnp.transpose(wide_ref[...])

    drow_ref[...] = jnp.zeros_like(drow_ref)
    mine = mat_t[pl.ds(pl.multiple_of(me * e_loc, e_loc), e_loc), :]
    pos = lax.broadcasted_iota(jnp.int32, (e_loc, SPAN), 1).astype(F32)
    slot0 = lax.broadcasted_iota(jnp.int32, (e_loc, SPAN), 0).astype(F32) * capacity
    for k in range(GROUP):
        kept_c, off_c, start_c, tot_c = (mine[:, r + k:r + k + 1] for r in (8, 16, 24, 32))

        def slots(p):
            inside = (p >= start_c) & (p < start_c + kept_c)
            return jnp.sum(jnp.where(inside, slot0 + off_c + p - start_c + 1.0, 0.0), axis=0, keepdims=True) - 1.0

        dl_ref[k:k + 1, :] = slots(pos)
        drow_ref[k:k + 1, :] = slots(pos - (SPAN - tot_c))
    dr_ref[...] = jnp.transpose(drow_ref[...])

    for k in range(1, GROUP):
        count_copy(k).wait_send()


def moe_kernel(plan, capacity, x_ref, qrow_ref, qcol_ref, dl_ref, dr_ref, w_in, w_out, y_ref,
               send, recv, rsend, rrecv, bbuf, obuf, got, acc, wi, wo, dlc, drc, tcol, trow, icol,
               s_send, s_recv, r_send, r_recv, wi_sem, wo_sem):
    nc, ns = plan.chunks, plan.slots
    rows = GROUP * ZROWS
    n_tok, d_model = x_ref.shape
    e_loc, _, ff = w_in.shape
    per_e = ff // FTILE
    quad = 4 * capacity
    where = position()

    def w_copies(i, slot):
        e, f = i // per_e, i % per_e
        cols = pl.ds(pl.multiple_of(f * FTILE, FTILE), FTILE)
        return (pltpu.make_async_copy(w_in.at[e, :, cols], wi.at[slot], wi_sem.at[slot]),
                pltpu.make_async_copy(w_out.at[e, cols, :], wo.at[slot], wo_sem.at[slot]))

    for i in range(ns):
        for copy in w_copies(i, i):
            copy.start()

    def out_copy(c, k):
        return pltpu.make_async_remote_copy(
            src_ref=send.at[c, k], dst_ref=recv.at[c, k], send_sem=s_send.at[c, k], recv_sem=s_recv.at[c, k],
            device_id=partner(where, k)[1], device_id_type=MESH)

    def back_copy(c, k):
        return pltpu.make_async_remote_copy(
            src_ref=rsend.at[c, k], dst_ref=rrecv.at[c, k], send_sem=r_send.at[c, k], recv_sem=r_recv.at[c, k],
            device_id=partner(where, k)[1], device_id_type=MESH)

    def targets(shape, dim):
        i = lax.broadcasted_iota(jnp.int32, shape, dim)
        k = jnp.zeros(shape, jnp.int32)
        for m in range(1, GROUP):
            k = k + jnp.where(i >= m * ZROWS, 1, 0)
        return (i + k * (SPAN - ZROWS)).astype(F32)

    tcol[...] = targets(tcol.shape, 0)
    trow[...] = targets(trow.shape, 1) + float(SPAN - nc * ZROWS)
    icol[...] = lax.broadcasted_iota(jnp.int32, icol.shape, 0).astype(F32)

    greet(where)

    def hot_of(a, b):
        return jnp.where(a == b, 1.0, 0.0).astype(BF16)

    @pl.loop(0, nc)
    def _(c):
        want = tcol[:, 0:1] + (c * ZROWS).astype(F32)
        packed = jnp.dot(hot_of(want, qrow_ref[0:1, :]), x_ref[...], preferred_element_type=F32).astype(BF16)
        send[c] = packed.reshape(GROUP, ZROWS, d_model)
        recv[c, 0] = send[c, 0]
        for k in range(GROUP - 1, 0, -1):
            out_copy(c, k).start()

    for c in range(nc):
        for k in range(GROUP):
            dlc[c, 0:1, k * ZROWS:(k + 1) * ZROWS] = dl_ref[k:k + 1, c * ZROWS:(c + 1) * ZROWS]
            first = SPAN - nc * ZROWS + c * ZROWS
            drc[c, k * ZROWS:(k + 1) * ZROWS, :] = dr_ref[first:first + ZROWS, k:k + 1]

    @pl.loop(0, 4)
    def _(g):
        @pl.loop(plan.need_lo(g), plan.need(g))
        def _(c):
            for k in range(1, GROUP):
                out_copy(c, k).wait_recv()

        acc[...] = jnp.zeros_like(acc)

        @pl.loop(0, plan.need(g))
        def _(c):
            slot_row = dlc[c, 0:1, :] - (g * quad).astype(F32)
            acc[...] += jnp.dot(hot_of(icol[:, 0:1], slot_row), recv[c].reshape(rows, d_model), preferred_element_type=F32)

        bbuf[...] = acc[...].astype(BF16)

        @pl.loop(0, 4)
        def _(j):
            e = g * 4 + j
            at = pl.ds(pl.multiple_of(j * capacity, capacity), capacity)
            total = None
            for f in range(per_e):
                i = e * per_e + f
                slot = i % ns
                for copy in w_copies(i, slot):
                    copy.wait()
                v = jnp.dot(bbuf[at, :], wi[slot], preferred_element_type=F32)
                h = 0.5 * v * (1.0 + jnp.tanh(0.7978845608028654 * (v + 0.044715 * (v * v * v))))
                part = jnp.dot(h.astype(BF16), wo[slot], preferred_element_type=F32)
                total = part if total is None else total + part

                @pl.when(i + ns < e_loc * per_e)
                def _():
                    for copy in w_copies(i + ns, slot):
                        copy.start()
            obuf[g, at, :] = total.astype(BF16)

        @pl.loop(plan.free_lo(g), plan.free(g))
        def _(c):
            acc[0:rows, :] = jnp.zeros((rows, d_model), F32)

            @pl.loop(0, g + 1)
            def _(m):
                slot_row = lax.broadcasted_iota(jnp.int32, (1, quad), 1).astype(F32) + (m * quad).astype(F32)
                acc[0:rows, :] += jnp.dot(hot_of(drc[c], slot_row), obuf[m], preferred_element_type=F32)

            rsend[c] = acc[0:rows, :].astype(BF16).reshape(GROUP, ZROWS, d_model)
            rrecv[c, 0] = rsend[c, 0]
            for k in range(GROUP - 1, 0, -1):
                back_copy(c, k).start()

    tt = 256
    got[...] = jnp.zeros_like(got)

    @pl.loop(0, nc)
    def _(c):
        for k in range(1, GROUP):
            back_copy(c, k).wait_recv()
        want = trow[0:1, :] + (c * ZROWS).astype(F32)

        @pl.loop(0, n_tok // tt)
        def _(t):
            at = pl.ds(pl.multiple_of(t * tt, tt), tt)
            got[at, :] += jnp.dot(hot_of(qcol_ref[at, 0:1], want), rrecv[c].reshape(rows, d_model),
                                  preferred_element_type=F32).astype(BF16)

    @pl.loop(0, n_tok // tt)
    def _(t):
        at = pl.ds(pl.multiple_of(t * tt, tt), tt)
        y_ref[at, :] = (x_ref[at, :].astype(F32) + qcol_ref[at, 1:2] * got[at, :].astype(F32)).astype(BF16)

    @pl.loop(0, nc)
    def _(c):
        for k in range(1, GROUP):
            out_copy(c, k).wait_send()
            back_copy(c, k).wait_send()


def solution(mesh):
    dev_axes = ('ep2', 'ep')

    def local_step(x_loc, ids_loc, gate_loc, w_a, w_b):
        n_tok, d_model = x_loc.shape
        e_loc, _, ff = w_a.shape
        experts = e_loc * GROUP
        capacity = 8 * ((5 * GROUP * n_tok) // (32 * experts))
        vmem = pl.BlockSpec(memory_space=pltpu.VMEM)
        hbm = pl.BlockSpec(memory_space=pl.ANY)

        qrow, qcol, dl, dr, sel = pl.pallas_call(
            functools.partial(route_kernel, capacity),
            out_shape=(jax.ShapeDtypeStruct((8, n_tok), F32), jax.ShapeDtypeStruct((n_tok, 128), F32),
                       jax.ShapeDtypeStruct((8, SPAN), F32), jax.ShapeDtypeStruct((SPAN, 128), F32),
                       jax.ShapeDtypeStruct((8, experts), jnp.int32)),
            in_specs=[vmem] * 2, out_specs=(vmem,) * 5,
            scratch_shapes=[
                pltpu.VMEM((GROUP, 8, experts), F32),
                pltpu.VMEM((8, experts), F32), pltpu.VMEM((8, experts), F32),
                pltpu.VMEM((8, experts), F32), pltpu.VMEM((8, experts), F32),
                pltpu.VMEM((128, experts), F32), pltpu.VMEM((experts, 128), F32),
                pltpu.VMEM((experts, n_tok), F32), pltpu.VMEM((128, n_tok), F32), pltpu.VMEM((128, SPAN), F32),
                pltpu.SemaphoreType.DMA((GROUP,)), pltpu.SemaphoreType.DMA((GROUP,)),
            ],
            compiler_params=pltpu.CompilerParams(collective_id=0, has_side_effects=True),
            name='route',
        )(ids_loc.reshape(1, n_tok), gate_loc.reshape(1, n_tok))

        def variant(number):
            plan = PLANS[number]
            nc, ns = plan.chunks, plan.slots
            rows = GROUP * ZROWS
            block = (nc, GROUP, ZROWS, d_model)

            def call(x_loc, qrow, qcol, dl, dr, w_a, w_b):
                return pl.pallas_call(
                    functools.partial(moe_kernel, plan, capacity),
                    out_shape=jax.ShapeDtypeStruct((n_tok, d_model), BF16),
                    in_specs=[vmem] * 5 + [hbm] * 2, out_specs=vmem,
                    scratch_shapes=[
                        pltpu.VMEM(block, BF16), pltpu.VMEM(block, BF16), pltpu.VMEM(block, BF16), pltpu.VMEM(block, BF16),
                        pltpu.VMEM((4 * capacity, d_model), BF16), pltpu.VMEM((4, 4 * capacity, d_model), BF16),
                        pltpu.VMEM((n_tok, d_model), BF16), pltpu.VMEM((4 * capacity, d_model), F32),
                        pltpu.VMEM((ns, d_model, FTILE), BF16), pltpu.VMEM((ns, FTILE, d_model), BF16),
                        pltpu.VMEM((nc, 8, rows), F32), pltpu.VMEM((nc, rows, 1), F32),
                        pltpu.VMEM((rows, 128), F32), pltpu.VMEM((8, rows), F32), pltpu.VMEM((4 * capacity, 128), F32),
                        pltpu.SemaphoreType.DMA((nc, GROUP)), pltpu.SemaphoreType.DMA((nc, GROUP)),
                        pltpu.SemaphoreType.DMA((nc, GROUP)), pltpu.SemaphoreType.DMA((nc, GROUP)),
                        pltpu.SemaphoreType.DMA((ns,)), pltpu.SemaphoreType.DMA((ns,)),
                    ],
                    compiler_params=pltpu.CompilerParams(
                        collective_id=1 + number, has_side_effects=True, vmem_limit_bytes=66_000_000),
                    name='moe_' + str(nc),
                )(x_loc, qrow, qcol, dl, dr, w_a, w_b)

            return call

        return lax.switch(sel[0, 0], [variant(i) for i in range(len(PLANS))], x_loc, qrow, qcol, dl, dr, w_a, w_b)

    tok_spec = P(('dp', 'ep2', 'ep'), None)
    w_spec = P(dev_axes, None, None)
    return jax.shard_map(local_step, mesh=mesh, in_specs=(tok_spec, tok_spec, tok_spec, w_spec, w_spec), out_specs=tok_spec, check_vma=False)
```

time: 387 us -> 142 us (0.37)
  local copies, waits for them, and re-layouts: 202 us -> 4.95 us
  Pallas kernels: 0 us -> 136 us
  waiting for transfers between devices: 81.5 us -> 0 us
  matrix products: 52.2 us -> 0 us
  other arithmetic: 31.6 us -> 0 us
  starting transfers between devices: 9.29 us -> 0 us
  blocking collectives: 8.82 us -> 0 us
    gather x15 -> x0, local copies, waits for them, and re-layouts: 154 us -> none  [the longest x3 35.9 us: expert_rows(): return out_rows.reshape(e_loc * capacity, d_model)[back_pos]]
    pallas_call x0 -> x2, Pallas kernels: none -> 136 us  [the longest x1 126 us: call(): pl.pallas_call(functools.partial(moe_kernel, plan, capacity), out_shape=j...]
    all_to_all x3 -> x0, waiting for transfers between devices: 81.5 us -> none  [the longest x1 57.4 us: local_step(): lax.all_to_all(send_rows.reshape(group_size, e_loc, lane_max, d_model), d...]
    dot_general x1 -> x0, matrix products: 52.2 us -> none  [expert_rows(): jnp.einsum('ecf,efd->ecd', hidden, w_b, preferred_element_type=jnp.float32)]
    all_to_all x3 -> x0, local copies, waits for them, and re-layouts: 15.6 us -> none  [the longest x1 7.75 us: local_step(): lax.all_to_all(send_rows.reshape(group_size, e_loc, lane_max, d_model), d...]
    scatter-add x1 -> x0, other arithmetic: 14.7 us -> none  [local_step(): counts = jnp.bincount(flat_e, length=experts)]
    all_to_all x3 -> x0, starting transfers between devices: 9.29 us -> none  [the longest x1 3.64 us: local_step(): lax.all_to_all(send_rows.reshape(group_size, e_loc, lane_max, d_model), d...]
    all_to_all x1 -> x0, blocking collectives: 8.82 us -> none  [local_step(): lax.all_to_all(counts.reshape(group_size, e_loc), dev_axes, 0, 0, tiled=T...]
  transfers between devices with their start and end apart: 3 -> 0, of which waited for: 2 -> 0; matrix products, arithmetic and copies ran while one was open for 16% -> 0% of each run, Pallas kernels for 0% -> 0%
where the time goes in v1:
time: 142 us
  Pallas kernels  136 us (96%)
  local copies, waits for them, and re-layouts  4.95 us (3%)
    pallas_call x1, Pallas kernels, call(): pl.pallas_call(functools.partial(moe_kernel, plan, capacity), out_shape=j...  126 us
    pallas_call x1, Pallas kernels, local_step(): pl.pallas_call(functools.partial(route_kernel, capacity), out_shape=(jax....  10.4 us
    unnamed x1, local copies, waits for them, and re-layouts  3.76 us

profile of v1, /device:TPU:0, one launch (start us, length us, event | category | flops | bytes accessed | tf_op | source)
XLA Modules:
  0.0 142.2 jit_solution(1813906190363149175)
XLA Ops:
  0.0 10.4 %route.1 = (f32[8,2048]{1,0:T(8,128)S(1)}, f32[2048,128]{1,0:T(8,128)}, f32[8,640]{1,0:T(8,128)S(1)}, f32[640,128]{1,0:T(8,128)S(1)}, s32[8,128]{1,0:T(8,128)}) custom-call(s32[1,2048]{1,0:T(1,128)} %bitcast.3, f32[1,2048]{1,0:T(1,128)} %bitcast.4), custom_call_target="tpu_custom_call" | custom-call | tf_op jit(solution)/shard_map/route/pallas_call | solution.py:321
  10.4 1.2 slice.3
  12.3 126.2 %conditional.1 = (bf16[2048,768]{1,0:T(8,128)(2,1)}) conditional(s32[]{:T(128)} %bitcast.2, (bf16[2048,768]{1,0:T(8,128)(2,1)}, f32[8,2048]{1,0:T(8,128)S(1)}, f32[2048,128]{1,0:T(8,128)}, f32[8,640]{1,0:T(8,128)S(1)}, f32[640,128]{1,0:T(8,128)S(1)}, /*index=5*/bf16[16,768,3072]{2,1,0:T(8,128)(2,1)}, ...), branch_computations={%region_0.0_spmd, %region_1.0_spmd, %region_2.0_spmd} | conditional | bytes 8 | solution.py:368
  12.3 126.0 %moe_7.1 = bf16[2048,768]{1,0:T(8,128)(2,1)} custom-call(bf16[2048,768]{1,0:T(8,128)(2,1)} %get-tuple-element.50.x_ref, f32[8,2048]{1,0:T(8,128)S(1)} %get-tuple-element.52.qrow_ref, f32[2048,128]{1,0:T(8,128)} %get-tuple-element.53.qcol_ref, f32[8,640]{1,0:T(8,128)S(1)} %get-tuple-element.54.dl_ref, f32[640,128]{1,0:T(8,128)S(1)} %get-tuple-element.55.dr_ref, ...), custom_call_target="tpu_custom_call" | custom-call | tf_op jit(solution)/shard_map/cond/branch_0_fun/moe_7/pallas_call | solution.py:346
  138.5 3.8 %copy.13 = bf16[2048,768]{1,0:T(8,128)(2,1)} copy(bf16[2048,768]{1,0:T(8,128)(2,1)} %get-tuple-element.82) | data formatting | bytes 6291456
